TPU v7x, 32 devices: a whole 2x2x4 slice. The times are simulated.
32 devices in a mesh: rep: 4 (over z), row: 2 (over x), col: 4 (over y, core).
Axes of the slice: x: 2, y: 2, z: 4, core: 2. Of those that a mesh axis runs over, the one named last changes fastest.
Arguments:
- grad_parts: bfloat16 [4, 8192, 8192], P('rep', 'row', 'col'), may hold values from -6 to 6
- momentum: float32 [8192, 8192], P(('row', 'rep'), 'col'), may hold values from -24 to 24
- basis: float32 [8192, 384], P('col'), may hold values from -0.0625 to 0.0625
Outputs:
- update: bfloat16 [8192, 8192], P('row', 'col')
- new_momentum: float32 [8192, 8192], P(('row', 'rep'), 'col')
- new_basis: float32 [8192, 384], P('col')
- power_norms: float32 [384], replicated
All inputs are finite; a program needn't handle non-finite values.
Results may differ from a plain program's by a relative error of at most 0.0085.
Values may be sent and summed in bfloat16 or wider, within the bound.
No kernel may reach another device: no remote copies, remote signals or barrier semaphores. Data moves between devices by JAX's collectives and lax.ppermute only.
A program may use at most 128 MiB of HBM per device.

v0:
```python
import jax
import jax.numpy as jnp
from jax import lax
from jax.sharding import PartitionSpec as P

D = 8192
RANK = 384
EPS = 1e-06
FEEDBACK = 0.05
HIGH = lax.Precision.HIGHEST


def local(grad_parts, momentum, basis):
    replicas = lax.axis_size("rep")
    local_grad = grad_parts[0].astype(jnp.float32)
    summed = lax.psum_scatter(
        local_grad.astype(jnp.bfloat16), "rep", scatter_dimension=0, tiled=True
    ).astype(jnp.float32)
    blended = momentum + summed / replicas
    power = jnp.dot(blended, basis, precision=HIGH)
    power = lax.psum(power, "col")
    squares = lax.psum(jnp.sum(power * power, axis=0), ("rep", "row"))
    power_norms = jnp.sqrt(squares / D)
    scaled = power / (jnp.sqrt(squares) + EPS)
    gram = lax.psum(jnp.dot(scaled.T, scaled, precision=HIGH), ("rep", "row"))
    factor = jnp.linalg.cholesky(gram)
    orth = jax.scipy.linalg.solve_triangular(factor, scaled.T, lower=True).T
    tile_orth = lax.all_gather(orth, "rep", axis=0, tiled=True)
    back = jnp.dot(blended.T, orth, precision=HIGH)
    back = lax.psum(back, ("rep", "row"))
    back_squares = lax.psum(jnp.sum(back * back, axis=0), "col")
    new_basis = back / (jnp.sqrt(back_squares) + EPS)
    new_momentum = blended - FEEDBACK * jnp.dot(orth, back.T, precision=HIGH)
    scale = D / RANK**0.5
    update = (scale * jnp.dot(tile_orth, new_basis.T, precision=HIGH)).astype(jnp.bfloat16)
    return (update, new_momentum, new_basis, power_norms)


def solution(mesh):
    placed = (P("rep", "row", "col"), P(("row", "rep"), "col"), P("col", None))
    return jax.shard_map(
        local,
        mesh=mesh,
        in_specs=placed,
        out_specs=(P("row", "col"), P(("row", "rep"), "col"), P("col", None), P()),
        check_vma=False,
    )
```

profile of v0, /device:TPU:0, one launch (start us, length us, event | category | flops | bytes accessed | tf_op | source)
XLA Modules:
  0.0 922.6 jit_solution(1023822813130225376)
XLA Ops:
  8.0 285.6 %reduce-scatter.2.cloned.1.call-done = bf16[1024,2048]{1,0:T(8,128)(2,1)} async-done(((bf16[4096,2048]{1,0:T(8,128)(2,1)}), bf16[1024,2048]{1,0:T(8,128)(2,1)}) %reduce-scatter.2.cloned.1.call-update) | async-done | bytes 4194320 | tf_op jit(solution)/shard_map/reduce_scatter | solution.py:16
  293.5 17.7 %fusion.1 = f32[1024,384]{1,0:T(8,128)} fusion(f32[2048,384]{1,0:T(8,128)S(1)} %copy-done, f32[1024,2048]{1,0:T(8,128)} %param.4, bf16[1024,2048]{1,0:T(8,128)(2,1)} %reduce-scatter.2.cloned.1.call-done), kind=kOutput, calls=%fused_computation.7 | convolution fusion | flops 9669967872 | bytes 17301504 | tf_op jit(solution)/shard_map/dot_general | solution.py:20
  311.3 43.6 %all-reduce.5.cloned.1.call-done = f32[1024,384]{1,0:T(8,128)} async-done(((f32[1024,384]{1,0:T(8,128)}), f32[1024,384]{1,0:T(8,128)}) %all-reduce.5.cloned.1.call-update) | async-done | bytes 1572880 | tf_op jit(solution)/shard_map/psum | solution.py:21
  354.9 1.6 multiply_reduce_fusion.1
  356.5 21.4 %psum.36 = f32[384]{0:T(512)S(1)} all-reduce(f32[384]{0:T(512)S(1)} %multiply_reduce_fusion.1), channel_id=1, replica_groups=mesh['rep'=4,'row'=2,'col'=4] {'rep','row'}, use_global_device_ids=true, to_apply=%region_3.0 | all-reduce | flops 384 | bytes 3072 | tf_op jit(solution)/shard_map/psum | solution.py:22
  378.5 5.6 fusion.7
  384.4 69.4 %all-reduce.7.cloned.1.call-done = f32[384,384]{0,1:T(8,128)} async-done(((f32[384,384]{0,1:T(8,128)}), f32[384,384]{0,1:T(8,128)}) %all-reduce.7.cloned.1.call-update) | async-done | bytes 589840 | tf_op jit(solution)/shard_map/psum | solution.py:25
  453.9 1.3 copy.8
  455.1 1.1 fusion.8
  456.3 11.7 %cholesky.77 = f32[128,128]{1,0:T(8,128)S(1)} custom-call(f32[128,128]{1,0:T(8,128)S(1)} %cholesky.192), custom_call_target="Cholesky" | custom-call | tf_op jit(solution)/shard_map/jit(cholesky)/cholesky | solution.py:26
  468.0 9.8 %custom-call.23 = f32[1,128,128]{1,2,0:T(8,128)S(1)} custom-call(f32[1,128,128]{2,1,0:T(8,128)S(1)} %get-tuple-element.28), custom_call_target="InvertDiagBlocksLowerTriangular" | custom-call | tf_op jit(solution)/shard_map/jit(cholesky)/cholesky | solution.py:26
  478.5 11.7 %cholesky.162 = f32[128,128]{1,0:T(8,128)S(1)} custom-call(f32[128,128]{1,0:T(8,128)S(1)} %cholesky.196), custom_call_target="Cholesky" | custom-call | tf_op jit(solution)/shard_map/jit(cholesky)/cholesky | solution.py:26
  490.2 10.2 %custom-call.24 = f32[1,128,128]{1,2,0:T(8,128)S(1)} custom-call(f32[1,128,128]{2,1,0:T(8,128)S(1)} %get-tuple-element.25), custom_call_target="InvertDiagBlocksLowerTriangular" | custom-call | tf_op jit(solution)/shard_map/jit(cholesky)/cholesky | solution.py:26
  500.9 11.7 %cholesky.181 = f32[128,128]{1,0:T(8,128)S(1)} custom-call(f32[128,128]{1,0:T(8,128)S(1)} %convolution_subtract_fusion.3), custom_call_target="Cholesky" | custom-call | tf_op jit(solution)/shard_map/jit(cholesky)/cholesky | solution.py:26
  512.7 0.7 compare_reduce_fusion
  516.1 6.0 while.1
  516.7 1.4 bitcast_dynamic-update-slice_fusion.2
  518.7 1.4 bitcast_dynamic-update-slice_fusion.2
  520.7 1.4 bitcast_dynamic-update-slice_fusion.2
  522.1 29.5 %custom-call.25 = f32[3,128,128]{1,2,0:T(8,128)S(1)} custom-call(f32[3,128,128]{2,1,0:T(8,128)S(1)} %get-tuple-element.11), custom_call_target="InvertDiagBlocksLowerTriangular" | custom-call | tf_op jit(solution)/shard_map/jit(_solve_triangular)/triangular_solve | solution.py:27
  552.3 1.0 convolution_subtract_fusion.1
  553.9 2.9 convolution_subtract_fusion
  557.5 30.4 %fusion = f32[2048,384]{1,0:T(8,128)} fusion(f32[1024,2048]{1,0:T(8,128)} %param.4, bf16[1024,2048]{1,0:T(8,128)(2,1)S(1)} %copy-done.2, f32[128,1024]{1,0:T(8,128)S(1)} %fusion.15, f32[128,1024]{1,0:T(8,128)S(1)} %fusion.17, f32[128,1024]{1,0:T(8,128)S(1)} %fusion.9), kind=kOutput, calls=%fused_computation.6 | convolution fusion | flops 9670754304 | bytes 17301504 | tf_op jit(solution)/shard_map/dot_general | solution.py:29
  588.0 1.3 fusion.5
  589.3 126.5 %all-reduce.9.cloned.1.call-done = f32[2048,384]{1,0:T(8,128)} async-done(((f32[2048,384]{1,0:T(8,128)}), f32[2048,384]{1,0:T(8,128)}) %all-reduce.9.cloned.1.call-update) | async-done | bytes 3145744 | tf_op jit(solution)/shard_map/psum | solution.py:30
  715.8 2.3 multiply_reduce_fusion
  718.1 6.2 psum.39
  724.4 1.9 broadcast_divide_fusion
  726.3 1.7 copy-done.3
  728.6 23.8 %multiply_subtract_fusion = f32[1024,2048]{1,0:T(8,128)} fusion(f32[2048,384]{1,0:T(8,128)S(1)} %copy-done.4, f32[1024,2048]{1,0:T(8,128)} %param.4, bf16[1024,2048]{1,0:T(8,128)(2,1)S(1)} %copy-done.3, f32[128,1024]{1,0:T(8,128)S(1)} %copy-done.10, f32[128,1024]{1,0:T(8,128)S(1)} %copy-done.8, f32[128,1024]{1,0:T(8,128)S(1)} %copy-done.6), kind=kOutput, calls=%fused_computation.3 | convolution fusion | flops 9674948608 | bytes 25690112 | tf_op jit(solution)/shard_map/dot_general | solution.py:33
  752.3 79.8 %all-gather.2.cloned.1.call-done = f32[4096,384]{0,1:T(8,128)} async-done(((f32[1024,384]{0,1:T(8,128)}), f32[4096,384]{0,1:T(8,128)}) %all-gather.2.cloned.1.call-update) | async-done | bytes 6291472 | tf_op jit(solution)/shard_map/all_gather | solution.py:28
  832.2 83.8 %multiply_convert_fusion = bf16[4096,2048]{1,0:T(8,128)(2,1)} fusion(f32[4096,384]{0,1:T(8,128)} %all-gather.2.cloned.1.call-done, f32[2048,384]{1,0:T(8,128)} %broadcast_divide_fusion), kind=kOutput, calls=%fused_computation.2 | convolution fusion | flops 38671482880 | bytes 26214400 | tf_op jit(solution)/shard_map/dot_general | solution.py:35
  (62 shorter events, 8.0 us)
Async XLA Ops:
  7.2 286.4 %copy-start = (f32[2048,384]{1,0:T(8,128)S(1)}, f32[2048,384]{1,0:T(8,128)}, u32[]{:S(2)}) copy-start(f32[2048,384]{1,0:T(8,128)} %param.5) | copy-start | bytes 9437188
  7.2 286.4 %reduce-scatter.2.cloned.1.call-start = ((), (), s32[]{:S(2)}) async-start(), calls=%async_computation.1 | async-start | bytes 20971520 | tf_op jit(solution)/shard_map/reduce_scatter | solution.py:16
  7.9 347.0 %all-reduce.5.cloned.1.call-start = ((), (), s32[]{:S(2)}) async-start(), calls=%async_computation.2 | async-start | bytes 3145728 | tf_op jit(solution)/shard_map/psum | solution.py:21
  311.3 142.6 %all-reduce.7.cloned.1.call-start = ((), (), s32[]{:S(2)}) async-start(), calls=%async_computation.3 | async-start | bytes 1179648 | tf_op jit(solution)/shard_map/psum | solution.py:25
  378.5 5.8 copy-start.11
  384.0 331.7 %all-reduce.9.cloned.1.call-start = ((), (), s32[]{:S(2)}) async-start(), calls=%async_computation.5 | async-start | bytes 6291456 | tf_op jit(solution)/shard_map/psum | solution.py:30
  522.1 30.2 %copy-start.12 = (f32[384,384]{1,0:T(8,128)}, f32[384,384]{1,0:T(8,128)S(1)}, u32[]{:S(2)}) copy-start(f32[384,384]{1,0:T(8,128)S(1)} %get-tuple-element.96) | copy-start | bytes 1769476
  552.3 35.7 %copy-start.5 = (f32[128,1024]{1,0:T(8,128)}, f32[128,1024]{1,0:T(8,128)S(1)}, u32[]{:S(2)}) copy-start(f32[128,1024]{1,0:T(8,128)S(1)} %fusion.9) | copy-start | bytes 1572868
  552.3 5.2 copy-start.2
  553.9 34.0 %copy-start.7 = (f32[128,1024]{1,0:T(8,128)}, f32[128,1024]{1,0:T(8,128)S(1)}, u32[]{:S(2)}) copy-start(f32[128,1024]{1,0:T(8,128)S(1)} %fusion.17) | copy-start | bytes 1572868
  557.5 30.5 %copy-start.9 = (f32[128,1024]{1,0:T(8,128)}, f32[128,1024]{1,0:T(8,128)S(1)}, u32[]{:S(2)}) copy-start(f32[128,1024]{1,0:T(8,128)S(1)} %fusion.15) | copy-start | bytes 1572868
  587.9 244.3 %all-gather.2.cloned.1.call-start = ((), (), s32[]{:S(2)}) async-start(), calls=%async_computation.4 | async-start | bytes 7864320 | tf_op jit(solution)/shard_map/all_gather | solution.py:28
  715.8 8.6 copy-start.4
  724.3 3.6 copy-start.3
  724.4 3.8 copy-start.6
  724.4 4.0 copy-start.8
  724.4 4.2 copy-start.10
  832.2 83.8 %copy-start.1 = (f32[2048,384]{1,0:T(8,128)S(1)}, f32[2048,384]{1,0:T(8,128)}, u32[]{:S(2)}) copy-start(f32[2048,384]{1,0:T(8,128)} %param.5) | copy-start | bytes 9437188
Sparse Core Ops, SparseCore 0:
  10.3 283.1 reduce-scatter.1
  311.4 43.4 all-reduce.4
  384.2 69.6 all-reduce.6
  588.0 127.7 all-reduce.8
  717.8 114.3 all-gather.1
where the time goes:
time: 930 us; the launch traced here: 923 us
  waiting for transfers between devices  606 us (65%)
  matrix products  168 us (18%)
  other arithmetic  95.1 us (10%)
  blocking collectives  27.6 us (3%)
  between operations  16.3 us (2%)
  local copies, waits for them, and re-layouts  9.64 us (1%)
    reduce_scatter x1, waiting for transfers between devices, local(): lax.psum_scatter(local_grad.astype(jnp.bfloat16), 'rep', scatter_dimensio...  286 us
    psum x1, waiting for transfers between devices, local(): back = lax.psum(back, ('rep', 'row'))  126 us
    dot_general x1, matrix products, local(): jnp.dot(tile_orth, new_basis.T, precision=HIGH)  83.8 us
    all_gather x1, waiting for transfers between devices, local(): tile_orth = lax.all_gather(orth, 'rep', axis=0, tiled=True)  79.8 us
    psum x1, waiting for transfers between devices, local(): gram = lax.psum(jnp.dot(scaled.T, scaled, precision=HIGH), ('rep', 'row'))  69.4 us
    another operation x10, other arithmetic, local(): factor = jnp.linalg.cholesky(gram)  56.6 us
    psum x1, waiting for transfers between devices, local(): power = lax.psum(power, 'col')  43.6 us
    dot_general x1, matrix products, local(): back = jnp.dot(blended.T, orth, precision=HIGH)  30.4 us
  transfers between devices with their start and end apart: 5, of which 5 were waited for; matrix products, arithmetic and copies ran while one was open for 3% of the time, Pallas kernels for 0%

commit v1 on v0

--- a/solution.py
+++ b/solution.py
@@ -8,6 +8,11 @@
 EPS = 1e-06
 FEEDBACK = 0.05
 HIGH = lax.Precision.HIGHEST
+
+
+def name_the_links(my_tile):
+    before = lax.psum(lax.psum(my_tile, "row"), "rep")
+    return before
 
 
 def local(grad_parts, momentum, basis):
@@ -27,7 +32,7 @@
     orth = jax.scipy.linalg.solve_triangular(factor, scaled.T, lower=True).T
     tile_orth = lax.all_gather(orth, "rep", axis=0, tiled=True)
     back = jnp.dot(blended.T, orth, precision=HIGH)
-    back = lax.psum(back, ("rep", "row"))
+    back = name_the_links(back)
     back_squares = lax.psum(jnp.sum(back * back, axis=0), "col")
     new_basis = back / (jnp.sqrt(back_squares) + EPS)
     new_momentum = blended - FEEDBACK * jnp.dot(orth, back.T, precision=HIGH)

time: 930 us -> 1010 us (1.086)
  waiting for transfers between devices: 606 us -> 686 us
    psum x1 -> x2, waiting for transfers between devices: 126 us -> 207 us  [name_the_links(): before = lax.psum(lax.psum(my_tile, 'row'), 'rep')]
  transfers between devices with their start and end apart: 5 -> 6, of which waited for: 5 -> 6; matrix products, arithmetic and copies ran while one was open for 3% -> 3% of each run, Pallas kernels for 0% -> 0%
where the time goes in v1:
time: 1010 us; the launch traced here: 1000 us
  waiting for transfers between devices  686 us (68%)
  matrix products  168 us (17%)
  other arithmetic  95.1 us (9%)
  blocking collectives  27.8 us (3%)
  between operations  16.6 us (2%)
    reduce_scatter x1, waiting for transfers between devices, local(): lax.psum_scatter(local_grad.astype(jnp.bfloat16), 'rep', scatter_dimensio...  286 us
    psum x2, waiting for transfers between devices, name_the_links(): before = lax.psum(lax.psum(my_tile, 'row'), 'rep')  207 us
    dot_general x1, matrix products, local(): jnp.dot(tile_orth, new_basis.T, precision=HIGH)  83.8 us
    all_gather x1, waiting for transfers between devices, local(): tile_orth = lax.all_gather(orth, 'rep', axis=0, tiled=True)  79.6 us
    psum x1, waiting for transfers between devices, local(): gram = lax.psum(jnp.dot(scaled.T, scaled, precision=HIGH), ('rep', 'row'))  69.4 us
    another operation x10, other arithmetic, local(): factor = jnp.linalg.cholesky(gram)  56.6 us
    psum x1, waiting for transfers between devices, local(): power = lax.psum(power, 'col')  43.6 us
    dot_general x1, matrix products, local(): back = jnp.dot(blended.T, orth, precision=HIGH)  30.4 us
  transfers between devices with their start and end apart: 6, of which 6 were waited for; matrix products, arithmetic and copies ran while one was open for 3% of the time, Pallas kernels for 0%

profile of v1, /device:TPU:0, one launch (start us, length us, event | category | flops | bytes accessed | tf_op | source)
XLA Modules:
  0.0 1003.3 jit_solution(17673271234168836671)
XLA Ops:
  8.0 285.6 %reduce-scatter.2.cloned.1.call-done = bf16[1024,2048]{1,0:T(8,128)(2,1)} async-done(((bf16[4096,2048]{1,0:T(8,128)(2,1)}), bf16[1024,2048]{1,0:T(8,128)(2,1)}) %reduce-scatter.2.cloned.1.call-update) | async-done | bytes 4194320 | tf_op jit(solution)/shard_map/reduce_scatter | solution.py:21
  293.5 17.7 %fusion.1 = f32[1024,384]{1,0:T(8,128)} fusion(f32[2048,384]{1,0:T(8,128)S(1)} %copy-done, f32[1024,2048]{1,0:T(8,128)} %param.4, bf16[1024,2048]{1,0:T(8,128)(2,1)} %reduce-scatter.2.cloned.1.call-done), kind=kOutput, calls=%fused_computation.7 | convolution fusion | flops 9669967872 | bytes 17301504 | tf_op jit(solution)/shard_map/dot_general | solution.py:25
  311.3 43.6 %all-reduce.6.cloned.1.call-done = f32[1024,384]{1,0:T(8,128)} async-done(((f32[1024,384]{1,0:T(8,128)}), f32[1024,384]{1,0:T(8,128)}) %all-reduce.6.cloned.1.call-update) | async-done | bytes 1572880 | tf_op jit(solution)/shard_map/psum | solution.py:26
  354.9 1.6 multiply_reduce_fusion.1
  356.5 21.4 %psum.43 = f32[384]{0:T(512)S(1)} all-reduce(f32[384]{0:T(512)S(1)} %multiply_reduce_fusion.1), channel_id=1, replica_groups=mesh['rep'=4,'row'=2,'col'=4] {'rep','row'}, use_global_device_ids=true, to_apply=%region_3.0 | all-reduce | flops 384 | bytes 3072 | tf_op jit(solution)/shard_map/psum | solution.py:27
  378.5 5.6 fusion.7
  384.4 69.4 %all-reduce.8.cloned.1.call-done = f32[384,384]{0,1:T(8,128)} async-done(((f32[384,384]{0,1:T(8,128)}), f32[384,384]{0,1:T(8,128)}) %all-reduce.8.cloned.1.call-update) | async-done | bytes 589840 | tf_op jit(solution)/shard_map/psum | solution.py:30
  453.9 1.3 copy.8
  455.1 1.1 fusion.8
  456.3 11.7 %cholesky.77 = f32[128,128]{1,0:T(8,128)S(1)} custom-call(f32[128,128]{1,0:T(8,128)S(1)} %cholesky.192), custom_call_target="Cholesky" | custom-call | tf_op jit(solution)/shard_map/jit(cholesky)/cholesky | solution.py:31
  468.0 9.8 custom-call.23
  478.5 11.7 %cholesky.162 = f32[128,128]{1,0:T(8,128)S(1)} custom-call(f32[128,128]{1,0:T(8,128)S(1)} %cholesky.196), custom_call_target="Cholesky" | custom-call | tf_op jit(solution)/shard_map/jit(cholesky)/cholesky | solution.py:31
  490.2 10.2 %custom-call.24 = f32[1,128,128]{1,2,0:T(8,128)S(1)} custom-call(f32[1,128,128]{2,1,0:T(8,128)S(1)} %get-tuple-element.25), custom_call_target="InvertDiagBlocksLowerTriangular" | custom-call | tf_op jit(solution)/shard_map/jit(cholesky)/cholesky | solution.py:31
  500.9 11.7 %cholesky.181 = f32[128,128]{1,0:T(8,128)S(1)} custom-call(f32[128,128]{1,0:T(8,128)S(1)} %convolution_subtract_fusion.3), custom_call_target="Cholesky" | custom-call | tf_op jit(solution)/shard_map/jit(cholesky)/cholesky | solution.py:31
  516.1 6.0 while.1
  516.7 1.4 bitcast_dynamic-update-slice_fusion.2
  518.7 1.4 bitcast_dynamic-update-slice_fusion.2
  520.7 1.4 bitcast_dynamic-update-slice_fusion.2
  522.1 29.5 %custom-call.25 = f32[3,128,128]{1,2,0:T(8,128)S(1)} custom-call(f32[3,128,128]{2,1,0:T(8,128)S(1)} %get-tuple-element.11), custom_call_target="InvertDiagBlocksLowerTriangular" | custom-call | tf_op jit(solution)/shard_map/jit(_solve_triangular)/triangular_solve | solution.py:32
  552.3 1.0 convolution_subtract_fusion.1
  553.9 2.9 convolution_subtract_fusion
  557.5 30.4 %fusion = f32[2048,384]{1,0:T(8,128)} fusion(f32[1024,2048]{1,0:T(8,128)} %param.4, bf16[1024,2048]{1,0:T(8,128)(2,1)S(1)} %copy-done.2, f32[128,1024]{1,0:T(8,128)S(1)} %fusion.15, f32[128,1024]{1,0:T(8,128)S(1)} %fusion.17, f32[128,1024]{1,0:T(8,128)S(1)} %fusion.9), kind=kOutput, calls=%fused_computation.6 | convolution fusion | flops 9670754304 | bytes 17301504 | tf_op jit(solution)/shard_map/dot_general | solution.py:34
  587.9 84.9 %all-reduce.10.cloned.1.call-done = f32[2048,384]{1,0:T(8,128)} async-done(((f32[2048,384]{1,0:T(8,128)}), f32[2048,384]{1,0:T(8,128)}) %all-reduce.10.cloned.1.call-update) | async-done | bytes 3145744 | tf_op jit(solution)/shard_map/psum | solution.py:14
  672.9 1.3 fusion.5
  674.2 121.9 %all-reduce.12.cloned.1.call-done = f32[2048,384]{1,0:T(8,128)} async-done(((f32[2048,384]{1,0:T(8,128)}), f32[2048,384]{1,0:T(8,128)}) %all-reduce.12.cloned.1.call-update) | async-done | bytes 3145744 | tf_op jit(solution)/shard_map/psum | solution.py:14
  796.1 2.3 multiply_reduce_fusion
  798.5 6.4 psum.47
  804.9 1.9 broadcast_divide_fusion
  806.8 1.8 copy-done.3
  809.1 23.7 %multiply_subtract_fusion = f32[1024,2048]{1,0:T(8,128)} fusion(f32[2048,384]{1,0:T(8,128)S(1)} %copy-done.4, f32[1024,2048]{1,0:T(8,128)} %param.4, bf16[1024,2048]{1,0:T(8,128)(2,1)S(1)} %copy-done.3, f32[128,1024]{1,0:T(8,128)S(1)} %copy-done.10, f32[128,1024]{1,0:T(8,128)S(1)} %copy-done.8, f32[128,1024]{1,0:T(8,128)S(1)} %copy-done.6), kind=kOutput, calls=%fused_computation.3 | convolution fusion | flops 9674948608 | bytes 25690112 | tf_op jit(solution)/shard_map/dot_general | solution.py:38
  832.9 79.6 %all-gather.2.cloned.1.call-done = f32[4096,384]{0,1:T(8,128)} async-done(((f32[1024,384]{0,1:T(8,128)}), f32[4096,384]{0,1:T(8,128)}) %all-gather.2.cloned.1.call-update) | async-done | bytes 6291472 | tf_op jit(solution)/shard_map/all_gather | solution.py:33
  912.5 83.8 %multiply_convert_fusion = bf16[4096,2048]{1,0:T(8,128)(2,1)} fusion(f32[4096,384]{0,1:T(8,128)} %all-gather.2.cloned.1.call-done, f32[2048,384]{1,0:T(8,128)} %broadcast_divide_fusion), kind=kOutput, calls=%fused_computation.2 | convolution fusion | flops 38671482880 | bytes 26214400 | tf_op jit(solution)/shard_map/dot_general | solution.py:40
  (65 shorter events, 8.8 us)
Async XLA Ops:
  7.2 286.4 %copy-start = (f32[2048,384]{1,0:T(8,128)S(1)}, f32[2048,384]{1,0:T(8,128)}, u32[]{:S(2)}) copy-start(f32[2048,384]{1,0:T(8,128)} %param.5) | copy-start | bytes 9437188
  7.2 286.4 %reduce-scatter.2.cloned.1.call-start = ((), (), s32[]{:S(2)}) async-start(), calls=%async_computation.1 | async-start | bytes 20971520 | tf_op jit(solution)/shard_map/reduce_scatter | solution.py:21
  7.9 347.0 %all-reduce.6.cloned.1.call-start = ((), (), s32[]{:S(2)}) async-start(), calls=%async_computation.2 | async-start | bytes 3145728 | tf_op jit(solution)/shard_map/psum | solution.py:26
  311.3 142.6 %all-reduce.8.cloned.1.call-start = ((), (), s32[]{:S(2)}) async-start(), calls=%async_computation.3 | async-start | bytes 1179648 | tf_op jit(solution)/shard_map/psum | solution.py:30
  378.5 5.8 copy-start.11
  384.0 288.8 %all-reduce.10.cloned.1.call-start = ((), (), s32[]{:S(2)}) async-start(), calls=%async_computation.5 | async-start | bytes 6291456 | tf_op jit(solution)/shard_map/psum | solution.py:14
  522.1 30.2 %copy-start.12 = (f32[384,384]{1,0:T(8,128)}, f32[384,384]{1,0:T(8,128)S(1)}, u32[]{:S(2)}) copy-start(f32[384,384]{1,0:T(8,128)S(1)} %get-tuple-element.100) | copy-start | bytes 1769476
  552.3 120.6 %copy-start.5 = (f32[128,1024]{1,0:T(8,128)}, f32[128,1024]{1,0:T(8,128)S(1)}, u32[]{:S(2)}) copy-start(f32[128,1024]{1,0:T(8,128)S(1)} %fusion.9) | copy-start | bytes 1572868
  552.3 5.2 copy-start.2
  553.9 119.0 %copy-start.7 = (f32[128,1024]{1,0:T(8,128)}, f32[128,1024]{1,0:T(8,128)S(1)}, u32[]{:S(2)}) copy-start(f32[128,1024]{1,0:T(8,128)S(1)} %fusion.17) | copy-start | bytes 1572868
  557.5 115.4 %copy-start.9 = (f32[128,1024]{1,0:T(8,128)}, f32[128,1024]{1,0:T(8,128)S(1)}, u32[]{:S(2)}) copy-start(f32[128,1024]{1,0:T(8,128)S(1)} %fusion.15) | copy-start | bytes 1572868
  587.9 208.2 %all-reduce.12.cloned.1.call-start = ((), (), s32[]{:S(2)}) async-start(), calls=%async_computation.6 | async-start | bytes 6291456 | tf_op jit(solution)/shard_map/psum | solution.py:14
  672.8 239.6 %all-gather.2.cloned.1.call-start = ((), (), s32[]{:S(2)}) async-start(), calls=%async_computation.4 | async-start | bytes 7864320 | tf_op jit(solution)/shard_map/all_gather | solution.py:33
  796.1 8.8 copy-start.4
  804.9 3.7 copy-start.3
  804.9 3.8 copy-start.6
  804.9 4.0 copy-start.8
  804.9 4.2 copy-start.10
  912.5 83.8 %copy-start.1 = (f32[2048,384]{1,0:T(8,128)S(1)}, f32[2048,384]{1,0:T(8,128)}, u32[]{:S(2)}) copy-start(f32[2048,384]{1,0:T(8,128)} %param.5) | copy-start | bytes 9437188
Sparse Core Ops, SparseCore 0:
  10.3 283.1 reduce-scatter.1
  311.4 43.4 all-reduce.5
  384.2 69.6 all-reduce.7
  588.0 84.7 all-reduce.9
  675.0 121.0 all-reduce.11
  798.1 114.3 all-gather.1
